TPU v7x, 32 devices: a whole 2x2x4 slice. The times are simulated.
32 devices in a mesh: layer: 8 (over y, x, core), tensor: 4 (over z).
Axes of the slice: x: 2, y: 2, z: 4, core: 2. Of those that a mesh axis runs over, the one named last changes fastest.
Arguments:
- gradient: bfloat16 [8, 1024, 8192], P(None, 'tensor', 'layer'), may hold values from -8 to 8
- row_basis: bfloat16 [8, 1024, 256], P('layer', 'tensor'), may hold values from -0.1875 to 0.1875
- column_basis: bfloat16 [8, 8192, 256], P('layer', 'tensor'), may hold values from -0.0625 to 0.0625
- row_eigen: float32 [8, 256], P('layer'), may hold values from 0.01 to 10
- column_eigen: float32 [8, 256], P('layer'), may hold values from 0.01 to 10
- row_escape: float32 [8], P('layer'), may hold values from 0.02 to 0.2
- column_escape: float32 [8], P('layer'), may hold values from 0.02 to 0.2
Outputs:
- update: bfloat16 [8, 1024, 8192], P(None, 'tensor', 'layer')
All inputs are finite; a program needn't handle non-finite values.
Results may differ from a plain program's by a relative error of at most 0.0055.
Values may be sent and summed in bfloat16 or wider, within the bound.
A program may use at most 128 MiB of HBM per device.

v0:
```python
import jax
import jax.numpy as jnp
from jax import lax
from jax.sharding import PartitionSpec as P


def coefficients(row_eigen, column_eigen, row_escape, column_escape):
    row_base = row_escape ** (-0.25)
    column_base = column_escape ** (-0.25)
    row_coef = (row_eigen + row_escape[:, None]) ** (-0.25) - row_base[:, None]
    column_coef = (column_eigen + column_escape[:, None]) ** (-0.25) - column_base[:, None]
    return (row_base, column_base, row_coef, column_coef)


def group_norm(local_block):
    partial_sq = jnp.sum(jnp.square(local_block.astype(jnp.float32)), axis=(1, 2))
    return lax.psum(partial_sq, "tensor")


def finish(raw_update, grad_sq):
    update_sq = lax.psum(jnp.sum(jnp.square(raw_update), axis=(1, 2)), "tensor")
    factor = jnp.sqrt((grad_sq + 1.0) / (update_sq + 1.0))
    return (raw_update * factor[:, None, None]).astype(jnp.bfloat16)


def body(gradient, row_basis, column_basis, row_eigen, column_eigen, row_escape, column_escape):
    row_base, column_base, row_coef, column_coef = coefficients(
        row_eigen, column_eigen, row_escape, column_escape
    )
    both_base = (row_base * column_base)[:, None, None]
    group_block = lax.all_to_all(gradient, "layer", split_axis=0, concat_axis=2, tiled=True)
    grad_sq = group_norm(group_block)
    own_proj = lax.psum_scatter(
        jnp.einsum(
            "lrk,lrd->dlk", row_basis, group_block, preferred_element_type=jnp.float32
        ).astype(jnp.bfloat16),
        "tensor",
        scatter_dimension=0,
        tiled=True,
    ).astype(jnp.float32)
    scaled = (own_proj * row_coef[None]).astype(jnp.bfloat16)
    core_part = jnp.einsum("dlk,ldj->lkj", scaled, column_basis, preferred_element_type=jnp.float32)
    core_mat = lax.psum(core_part.astype(jnp.bfloat16), "tensor")
    whole_columns = lax.all_gather(column_basis, "tensor", axis=1, tiled=True)
    middle = jnp.einsum(
        "lrd,ldk->lrk", group_block, whole_columns, preferred_element_type=jnp.float32
    )
    row_term = jnp.einsum(
        "lrk,dlk->lrd",
        row_basis,
        lax.all_gather(scaled, "tensor", axis=0, tiled=True),
        preferred_element_type=jnp.float32,
    )
    mixed = row_base[:, None, None] * middle + jnp.einsum(
        "lrk,lkj->lrj", row_basis, core_mat, preferred_element_type=jnp.float32
    )
    left_factor = (mixed * column_coef[:, None, :]).astype(jnp.bfloat16)
    raw_update = both_base * group_block.astype(jnp.float32) + column_base[:, None, None] * row_term
    raw_update = raw_update + jnp.einsum(
        "lrk,ldk->lrd", left_factor, whole_columns, preferred_element_type=jnp.float32
    )
    rows_block = finish(raw_update, grad_sq)
    return lax.all_to_all(rows_block, "layer", split_axis=2, concat_axis=0, tiled=True)


def solution(mesh):
    in_specs = (
        P(None, "tensor", "layer"),
        P("layer", "tensor", None),
        P("layer", "tensor", None),
        P("layer", None),
        P("layer", None),
        P("layer"),
        P("layer"),
    )
    out_specs = P(None, "tensor", "layer")
    return jax.shard_map(body, mesh=mesh, in_specs=in_specs, out_specs=out_specs, check_vma=False)
```

profile of v0, /device:TPU:0, one launch (start us, length us, event | category | flops | bytes accessed | tf_op | source)
XLA Modules:
  0.0 558.4 jit_solution(9425964493506922182)
XLA Ops:
  6.5 0.0 copy-start
  6.5 0.0 reduce-scatter.2.cloned.1.call-start
  6.5 54.5 %all_to_all.36 = bf16[8,256,1024]{2,1,0:T(8,128)(2,1)} all-to-all(bf16[8,256,1024]{2,1,0:T(8,128)(2,1)} %param.7), channel_id=1, replica_groups=mesh['layer'=8,'tensor'=4] {'layer'}, dimensions={0} | all-to-all | bytes 8388608 | tf_op jit(solution)/shard_map/all_to_all | solution.py:31
  61.0 6.4 %copy.15 = bf16[1,256,8,1024]{1,3,2,0:T(8,128)(2,1)} copy(bf16[1,256,8,1024]{3,1,2,0:T(8,128)(2,1)} %bitcast.80) | data formatting | bytes 8388608 | tf_op jit(solution)/shard_map/all_to_all | solution.py:31
  67.4 0.0 copy-done
  67.4 5.4 fusion.2
  72.8 0.0 copy-start.4
  72.8 0.0 copy-start.5
  72.8 0.0 reduce-scatter.2.cloned.1.call-update
  72.9 0.0 all-gather.5.cloned.1.call-start
  72.9 0.7 all-gather.5.cloned.1.call-update
  73.6 0.0 all-gather.3.cloned.1.call-start
  74.4 0.0 copy-done.4
  74.4 75.4 %reduce-scatter.2.cloned.1.call-done = bf16[2048,1,256]{2,0,1:T(8,128)(2,1)} async-done(((bf16[8192,1,256]{2,0,1:T(8,128)(2,1)}), bf16[2048,1,256]{2,0,1:T(8,128)(2,1)}) %reduce-scatter.2.cloned.1.call-update) | async-done | bytes 1048592 | tf_op jit(solution)/shard_map/reduce_scatter | solution.py:33
  149.8 2.4 multiply_convert_fusion.1
  152.2 0.0 all-gather.3.cloned.1.call-update
  152.3 0.0 all-reduce.3.cloned.1.call-start
  153.0 0.0 copy-done.5
  153.0 4.9 multiply_reduce_fusion.1
  157.9 0.0 copy-start.2
  158.0 0.0 copy-start.3
  158.0 74.7 %all-gather.5.cloned.1.call-done = bf16[1,8192,256]{2,1,0:T(8,128)(2,1)} async-done(((bf16[1,2048,256]{2,1,0:T(8,128)(2,1)}), bf16[1,8192,256]{2,1,0:T(8,128)(2,1)}) %all-gather.5.cloned.1.call-update) | async-done | bytes 4194320 | tf_op jit(solution)/shard_map/all_gather | solution.py:44
  232.7 4.8 fusion.10
  237.4 0.0 copy-done.2
  237.4 0.0 copy-done.3
  237.5 1.1 convolution_convert_fusion.1
  238.6 0.0 all-reduce.3.cloned.1.call-update
  238.6 75.0 %all-gather.3.cloned.1.call-done = bf16[8192,1,256]{2,0,1:T(8,128)(2,1)} async-done(((bf16[2048,1,256]{2,0,1:T(8,128)(2,1)}), bf16[8192,1,256]{2,0,1:T(8,128)(2,1)}) %all-gather.3.cloned.1.call-update) | async-done | bytes 4194320 | tf_op jit(solution)/shard_map/all_gather | solution.py:51
  313.6 8.0 %fusion.1 = f32[256,8192]{0,1:T(8,128)} fusion(bf16[256,8192]{0,1:T(8,128)(2,1)} %bitcast.79, bf16[8192,1,256]{2,0,1:T(8,128)(2,1)} %all-gather.3.cloned.1.call-done, f32[]{:T(128)} %bitcast.4, f32[]{:T(128)} %bitcast, bf16[1,256,256]{2,1,0:T(8,128)(2,1)S(1)} %copy-done), kind=kOutput, calls=%fused_computation.3 | convolution fusion | flops 1082130432 | bytes 16908296 | tf_op jit(solution)/shard_map/lrk,dlk->lrd/dot_general | solution.py:48
  321.6 27.3 %all-reduce.3.cloned.1.call-done = bf16[256,256]{1,0:T(8,128)(2,1)} async-done(((bf16[256,256]{1,0:T(8,128)(2,1)}), bf16[256,256]{1,0:T(8,128)(2,1)}) %all-reduce.3.cloned.1.call-update) | async-done | bytes 131088 | tf_op jit(solution)/shard_map/psum | solution.py:43
  348.9 11.0 %multiply_reduce_fusion = (f32[]{:T(128)}, f32[256,8192]{0,1:T(8,128)}) fusion(f32[256,8192]{0,1:T(8,128)} %fusion.1, bf16[1,8192,256]{2,1,0:T(8,128)(2,1)} %all-gather.5.cloned.1.call-done, f32[256,256]{1,0:T(8,128)S(1)} %fusion.10, bf16[256,256]{1,0:T(8,128)(2,1)} %all-reduce.3.cloned.1.call-done, bf16[1,256,256]{2,1,0:T(8,128)(2,1)S(1)} %copy-done, ...), kind=kOutput, calls=%fused_computation.7 | convolution fusion | flops 1113784320 | bytes 21496836 | tf_op jit(solution)/shard_map/lrk,ldk->lrd/dot_general | solution.py:59
  359.9 11.3 %all-reduce = (f32[1]{0:T(128)}, f32[1]{0:T(128)}) all-reduce(f32[1]{0:T(128)} %bitcast.19, f32[1]{0:T(128)} %bitcast.20), channel_id=1, replica_groups=mesh['layer'=8,'tensor'=4] {'tensor'}, use_global_device_ids=true, to_apply=%region_3.0 | all-reduce | flops 2 | bytes 16 | tf_op jit(solution)/shard_map/psum | solution.py:17
  372.5 4.1 fusion.3
  376.5 49.5 %copy.24 = bf16[1,256,8192]{1,0,2:T(2,128)(2,1)} copy(bf16[1,256,8192]{1,2,0:T(8,128)(2,1)S(1)} %fusion.3) | data formatting | bytes 8388608 | tf_op jit(solution)/shard_map/convert_element_type | solution.py:23
  426.1 0.5 broadcast.23
  426.6 43.5 %reduce.4 = bf16[8192,256]{1,0:T(8,128)(2,1)} reduce(bf16[8192,1,256]{2,1,0:T(2,128)(2,1)} %bitcast.81, bf16[]{:T(256)} %broadcast.23), dimensions={1}, to_apply=%bitcast.74.reduce_sub_computation | reduce | bytes 8388610
  470.1 7.0 %reshape.90 = bf16[8,2,131072]{2,1,0:T(2,128)(2,1)} reshape(bf16[8192,256]{1,0:T(8,128)(2,1)} %reduce.4) | data formatting | bytes 8388608
  477.1 53.6 %all_to_all.37 = bf16[8,2,131072]{2,1,0:T(2,128)(2,1)} all-to-all(bf16[8,2,131072]{2,1,0:T(2,128)(2,1)} %reshape.90), channel_id=1, replica_groups=mesh['layer'=8,'tensor'=4] {'layer'}, dimensions={0} | all-to-all | bytes 8388608 | tf_op jit(solution)/shard_map/all_to_all | solution.py:63
  530.6 8.7 %reshape.91 = bf16[8192,1,256]{2,1,0:T(2,128)(2,1)} reshape(bf16[8,2,131072]{2,1,0:T(2,128)(2,1)} %all_to_all.37) | data formatting | bytes 8388608
  539.4 6.1 %copy.22 = bf16[1,256,8192]{1,2,0:T(8,128)(2,1)} copy(bf16[1,256,8192]{1,0,2:T(2,128)(2,1)} %bitcast.82) | data formatting | bytes 8388608
  545.4 0.0 copy-start.1
  545.4 6.5 %copy.19 = bf16[8,256,1024]{2,1,0:T(8,128)(2,1)} copy(bf16[8,256,1024]{1,2,0:T(8,128)(2,1)} %bitcast.83) | data formatting | bytes 8388608 | tf_op jit(solution)/shard_map/all_to_all | solution.py:63
  551.9 0.0 copy-done.1
  (2 shorter events, 0.0 us)
Async XLA Ops:
  6.5 60.9 %copy-start = (bf16[1,256,256]{2,1,0:T(8,128)(2,1)S(1)}, bf16[1,256,256]{2,1,0:T(8,128)(2,1)}, u32[]{:S(2)}) copy-start(bf16[1,256,256]{2,1,0:T(8,128)(2,1)} %param.8) | copy-start | bytes 393220
  6.5 143.3 %reduce-scatter.2.cloned.1.call-start = ((), (), s32[]{:S(2)}) async-start(), calls=%async_computation.3 | async-start | bytes 5242880 | tf_op jit(solution)/shard_map/reduce_scatter | solution.py:33
  72.8 1.5 copy-start.4
  72.8 80.2 %copy-start.5 = (f32[1,256]{1,0:T(1,128)S(1)}, f32[1,256]{1,0:T(1,128)}, u32[]{:S(2)}) copy-start(f32[1,256]{1,0:T(1,128)} %param.11) | copy-start | bytes 3076
  72.9 159.8 %all-gather.5.cloned.1.call-start = ((), (), s32[]{:S(2)}) async-start(), calls=%async_computation.5 | async-start | bytes 5242880 | tf_op jit(solution)/shard_map/all_gather | solution.py:44
  73.6 239.9 %all-gather.3.cloned.1.call-start = ((), (), s32[]{:S(2)}) async-start(), calls=%async_computation.4 | async-start | bytes 5242880 | tf_op jit(solution)/shard_map/all_gather | solution.py:51
  152.3 196.6 %all-reduce.3.cloned.1.call-start = ((), (), s32[]{:S(2)}) async-start(), calls=%async_computation.6 | async-start | bytes 262144 | tf_op jit(solution)/shard_map/psum | solution.py:43
  157.9 79.5 %copy-start.2 = (bf16[2048,1,256]{2,0,1:T(8,128)(2,1)S(1)}, bf16[2048,1,256]{2,0,1:T(8,128)(2,1)}, u32[]{:S(2)}) copy-start(bf16[2048,1,256]{2,0,1:T(8,128)(2,1)} %multiply_convert_fusion.1) | copy-start | bytes 3145732
  158.0 79.5 %copy-start.3 = (bf16[1,2048,256]{2,1,0:T(8,128)(2,1)S(1)}, bf16[1,2048,256]{2,1,0:T(8,128)(2,1)}, u32[]{:S(2)}) copy-start(bf16[1,2048,256]{2,1,0:T(8,128)(2,1)} %param.9) | copy-start | bytes 3145732
  545.4 6.5 %copy-start.1 = (bf16[1,256,256]{2,1,0:T(8,128)(2,1)S(1)}, bf16[1,256,256]{2,1,0:T(8,128)(2,1)}, u32[]{:S(2)}) copy-start(bf16[1,256,256]{2,1,0:T(8,128)(2,1)} %param.8) | copy-start | bytes 393220
Sparse Core Ops, SparseCore 0:
  73.0 76.7 reduce-scatter.1
  151.4 81.2 all-gather.4
  234.3 79.2 all-gather.2
  315.7 33.1 all-reduce.2
where the time goes:
time: 559 us; the launch traced here: 558 us
  waiting for transfers between devices  253 us (45%)
  blocking collectives  119 us (21%)
  local copies, waits for them, and re-layouts  84.7 us (15%)
  other arithmetic  54.9 us (10%)
  matrix products  30.3 us (5%)
  between operations  15.9 us (3%)
    reduce_scatter x1, waiting for transfers between devices, body(): lax.psum_scatter(jnp.einsum('lrk,lrd->dlk', row_basis, group_block, prefe...  75.4 us
    all_gather x1, waiting for transfers between devices, body(): lax.all_gather(scaled, 'tensor', axis=0, tiled=True)  75 us
    all_gather x1, waiting for transfers between devices, body(): whole_columns = lax.all_gather(column_basis, 'tensor', axis=1, tiled=True)  74.7 us
    all_to_all x1, blocking collectives, body(): lax.all_to_all(gradient, 'layer', split_axis=0, concat_axis=2, tiled=True)  54.5 us
    all_to_all x1, blocking collectives, body(): lax.all_to_all(rows_block, 'layer', split_axis=2, concat_axis=0, tiled=True)  53.6 us
    convert_element_type x1, local copies, waits for them, and re-layouts, finish(): return (raw_update * factor[:, None, None]).astype(jnp.bfloat16)  49.5 us
    unnamed x1, other arithmetic  43.5 us
    psum x1, waiting for transfers between devices, body(): core_mat = lax.psum(core_part.astype(jnp.bfloat16), 'tensor')  27.3 us
  transfers between devices with their start and end apart: 4, of which 4 were waited for; matrix products, arithmetic and copies ran while one was open for 4% of the time, Pallas kernels for 0%

commit v1 on v0

--- a/solution.py
+++ b/solution.py
@@ -60,7 +60,16 @@
         "lrk,ldk->lrd", left_factor, whole_columns, preferred_element_type=jnp.float32
     )
     rows_block = finish(raw_update, grad_sq)
-    return lax.all_to_all(rows_block, "layer", split_axis=2, concat_axis=0, tiled=True)
+    _balance_frame = lambda v0: jnp.concatenate(
+        lax.all_to_all(
+            jnp.stack(jnp.split(v0, lax.axis_size("layer"), axis=2)),
+            axis_name="layer",
+            split_axis=0,
+            concat_axis=0,
+        ),
+        axis=0,
+    )
+    return _balance_frame(rows_block)
 
 
 def solution(mesh):

time: 559 us -> 443 us (0.79)
  local copies, waits for them, and re-layouts: 84.7 us -> 13.2 us
  other arithmetic: 54.9 us -> 11.5 us
    convert_element_type x1 -> x0, local copies, waits for them, and re-layouts: 49.5 us -> none  [finish(): return (raw_update * factor[:, None, None]).astype(jnp.bfloat16)]
    unnamed x1 -> x0, other arithmetic: 43.5 us -> none
    unnamed x16 -> x17, local copies, waits for them, and re-layouts: 22.3 us -> 0.27 us
    all_to_all x1 -> x0, local copies, waits for them, and re-layouts: 6.46 us -> none  [body(): lax.all_to_all(rows_block, 'layer', split_axis=2, concat_axis=0, tiled=True)]
    reshape x0 -> x1, local copies, waits for them, and re-layouts: none -> 6.43 us  [body(): jnp.concatenate(lax.all_to_all(jnp.stack(jnp.split(v0, lax.axis_size('lay...]
  transfers between devices with their start and end apart: 4 -> 4, of which waited for: 4 -> 4; matrix products, arithmetic and copies ran while one was open for 4% -> 5% of each run, Pallas kernels for 0% -> 0%
where the time goes in v1:
time: 443 us; the launch traced here: 442 us
  waiting for transfers between devices  253 us (57%)
  blocking collectives  118 us (27%)
  matrix products  30.3 us (7%)
  between operations  16.1 us (4%)
  local copies, waits for them, and re-layouts  13.2 us (3%)
  other arithmetic  11.5 us (3%)
    reduce_scatter x1, waiting for transfers between devices, body(): lax.psum_scatter(jnp.einsum('lrk,lrd->dlk', row_basis, group_block, prefe...  75.4 us
    all_gather x1, waiting for transfers between devices, body(): lax.all_gather(scaled, 'tensor', axis=0, tiled=True)  75 us
    all_gather x1, waiting for transfers between devices, body(): whole_columns = lax.all_gather(column_basis, 'tensor', axis=1, tiled=True)  74.6 us
    all_to_all x1, blocking collectives, body(): lax.all_to_all(gradient, 'layer', split_axis=0, concat_axis=2, tiled=True)  54.5 us
    all_to_all x1, blocking collectives, body(): lax.all_to_all(jnp.stack(jnp.split(v0, lax.axis_size('layer'), axis=2)),...  52.6 us
    psum x1, waiting for transfers between devices, body(): core_mat = lax.psum(core_part.astype(jnp.bfloat16), 'tensor')  27.3 us
    psum x1, blocking collectives, group_norm(): return lax.psum(partial_sq, 'tensor')  11.2 us
    dot_general x1, matrix products, body(): jnp.einsum('lrk,ldk->lrd', left_factor, whole_columns, preferred_element_...  11 us
  transfers between devices with their start and end apart: 4, of which 4 were waited for; matrix products, arithmetic and copies ran while one was open for 5% of the time, Pallas kernels for 0%

profile of v1, /device:TPU:0, one launch (start us, length us, event | category | flops | bytes accessed | tf_op | source)
XLA Modules:
  0.0 442.3 jit_solution(13179299295354182582)
XLA Ops:
  6.5 0.0 copy-start
  6.5 0.0 reduce-scatter.2.cloned.1.call-start
  6.5 54.5 %all_to_all.23 = bf16[8,256,1024]{2,1,0:T(8,128)(2,1)} all-to-all(bf16[8,256,1024]{2,1,0:T(8,128)(2,1)} %param.7), channel_id=1, replica_groups=mesh['layer'=8,'tensor'=4] {'layer'}, dimensions={0} | all-to-all | bytes 8388608 | tf_op jit(solution)/shard_map/all_to_all | solution.py:31
  61.0 6.4 %copy.8 = bf16[1,256,8,1024]{1,3,2,0:T(8,128)(2,1)} copy(bf16[1,256,8,1024]{3,1,2,0:T(8,128)(2,1)} %bitcast.104) | data formatting | bytes 8388608 | tf_op jit(solution)/shard_map/all_to_all | solution.py:31
  67.4 0.0 copy-done
  67.4 5.4 %fusion.2 = bf16[8192,1,256]{2,0,1:T(8,128)(2,1)} fusion(bf16[256,8192]{0,1:T(8,128)(2,1)} %bitcast.101, bf16[1,256,256]{2,1,0:T(8,128)(2,1)S(1)} %copy-done), kind=kOutput, calls=%fused_computation.5 | convolution fusion | flops 1075838976 | bytes 8519680 | tf_op jit(solution)/shard_map/lrk,lrd->dlk/dot_general | solution.py:34
  72.8 0.0 copy-start.3
  72.8 0.0 copy-start.4
  72.8 0.0 reduce-scatter.2.cloned.1.call-update
  72.9 0.0 all-gather.5.cloned.1.call-start
  72.9 0.7 all-gather.5.cloned.1.call-update
  73.6 0.0 all-gather.3.cloned.1.call-start
  74.4 0.0 copy-done.3
  74.4 75.4 %reduce-scatter.2.cloned.1.call-done = bf16[2048,1,256]{2,0,1:T(8,128)(2,1)} async-done(((bf16[8192,1,256]{2,0,1:T(8,128)(2,1)}), bf16[2048,1,256]{2,0,1:T(8,128)(2,1)}) %reduce-scatter.2.cloned.1.call-update) | async-done | bytes 1048592 | tf_op jit(solution)/shard_map/reduce_scatter | solution.py:33
  149.8 2.4 multiply_convert_fusion.1
  152.2 0.0 all-gather.3.cloned.1.call-update
  152.3 0.0 all-reduce.3.cloned.1.call-start
  153.0 0.0 copy-done.4
  153.0 5.0 %multiply_reduce_fusion.1 = f32[]{:T(128)} fusion(bf16[8,256,1024]{2,1,0:T(8,128)(2,1)} %all_to_all.23), kind=kLoop, calls=%fused_computation.8 | loop fusion | flops 6291455 | bytes 4194308 | tf_op jit(solution)/shard_map/reduce_sum | solution.py:16
  158.1 0.0 copy-start.1
  158.1 0.0 copy-start.2
  158.1 74.6 %all-gather.5.cloned.1.call-done = bf16[1,8192,256]{2,1,0:T(8,128)(2,1)} async-done(((bf16[1,2048,256]{2,1,0:T(8,128)(2,1)}), bf16[1,8192,256]{2,1,0:T(8,128)(2,1)}) %all-gather.5.cloned.1.call-update) | async-done | bytes 4194320 | tf_op jit(solution)/shard_map/all_gather | solution.py:44
  232.7 4.8 %fusion.10 = f32[256,256]{1,0:T(8,128)S(1)} fusion(bf16[256,8192]{0,1:T(8,128)(2,1)} %bitcast.102, bf16[1,8192,256]{2,1,0:T(8,128)(2,1)} %all-gather.5.cloned.1.call-done, f32[]{:T(128)} %bitcast.8), kind=kOutput, calls=%fused_computation.18 | convolution fusion | flops 1073807360 | bytes 8650756 | tf_op jit(solution)/shard_map/lrd,ldk->lrk/dot_general | solution.py:45
  237.4 0.0 copy-done.1
  237.4 0.0 copy-done.2
  237.4 1.1 convolution_convert_fusion.1
  238.6 0.0 all-reduce.3.cloned.1.call-update
  238.6 75.0 %all-gather.3.cloned.1.call-done = bf16[8192,1,256]{2,0,1:T(8,128)(2,1)} async-done(((bf16[2048,1,256]{2,0,1:T(8,128)(2,1)}), bf16[8192,1,256]{2,0,1:T(8,128)(2,1)}) %all-gather.3.cloned.1.call-update) | async-done | bytes 4194320 | tf_op jit(solution)/shard_map/all_gather | solution.py:51
  313.6 8.0 %fusion.1 = f32[256,8192]{0,1:T(8,128)} fusion(bf16[256,8192]{0,1:T(8,128)(2,1)} %bitcast.103, bf16[8192,1,256]{2,0,1:T(8,128)(2,1)} %all-gather.3.cloned.1.call-done, f32[]{:T(128)} %bitcast.4, f32[]{:T(128)} %bitcast, bf16[1,256,256]{2,1,0:T(8,128)(2,1)S(1)} %copy-done), kind=kOutput, calls=%fused_computation.3 | convolution fusion | flops 1082130432 | bytes 16908296 | tf_op jit(solution)/shard_map/lrk,dlk->lrd/dot_general | solution.py:48
  321.6 27.3 %all-reduce.3.cloned.1.call-done = bf16[256,256]{1,0:T(8,128)(2,1)} async-done(((bf16[256,256]{1,0:T(8,128)(2,1)}), bf16[256,256]{1,0:T(8,128)(2,1)}) %all-reduce.3.cloned.1.call-update) | async-done | bytes 131088 | tf_op jit(solution)/shard_map/psum | solution.py:43
  348.9 11.0 %multiply_reduce_fusion = (f32[]{:T(128)}, f32[256,8192]{0,1:T(8,128)}) fusion(f32[256,8192]{0,1:T(8,128)} %fusion.1, bf16[1,8192,256]{2,1,0:T(8,128)(2,1)} %all-gather.5.cloned.1.call-done, f32[256,256]{1,0:T(8,128)S(1)} %fusion.10, bf16[256,256]{1,0:T(8,128)(2,1)} %all-reduce.3.cloned.1.call-done, bf16[1,256,256]{2,1,0:T(8,128)(2,1)S(1)} %copy-done, ...), kind=kOutput, calls=%fused_computation.7 | convolution fusion | flops 1113784320 | bytes 21496836 | tf_op jit(solution)/shard_map/lrk,ldk->lrd/dot_general | solution.py:59
  359.9 11.2 %all-reduce = (f32[1]{0:T(128)}, f32[1]{0:T(128)}) all-reduce(f32[1]{0:T(128)} %bitcast.19, f32[1]{0:T(128)} %bitcast.20), channel_id=1, replica_groups=mesh['layer'=8,'tensor'=4] {'tensor'}, use_global_device_ids=true, to_apply=%region_3.0 | all-reduce | flops 2 | bytes 16 | tf_op jit(solution)/shard_map/psum | solution.py:17
  372.4 4.1 fusion.3
  376.8 52.6 %all_to_all.24 = bf16[8,1,256,1024]{2,3,1,0:T(8,128)(2,1)} all-to-all(bf16[8,1,256,1024]{2,3,1,0:T(8,128)(2,1)S(1)} %fusion.16), channel_id=1, replica_groups=mesh['layer'=8,'tensor'=4] {'layer'}, dimensions={0} | all-to-all | bytes 8388608 | tf_op jit(solution)/shard_map/all_to_all | solution.py:64
  429.4 6.4 %copy.10 = bf16[8,256,1024]{2,1,0:T(8,128)(2,1)} copy(bf16[8,256,1024]{1,2,0:T(8,128)(2,1)} %bitcast.105) | data formatting | bytes 8388608 | tf_op jit(solution)/shard_map/reshape | solution.py:63
  (10 shorter events, 0.3 us)
Async XLA Ops:
  6.5 60.9 %copy-start = (bf16[1,256,256]{2,1,0:T(8,128)(2,1)S(1)}, bf16[1,256,256]{2,1,0:T(8,128)(2,1)}, u32[]{:S(2)}) copy-start(bf16[1,256,256]{2,1,0:T(8,128)(2,1)} %param.8) | copy-start | bytes 393220
  6.5 143.3 %reduce-scatter.2.cloned.1.call-start = ((), (), s32[]{:S(2)}) async-start(), calls=%async_computation.3 | async-start | bytes 5242880 | tf_op jit(solution)/shard_map/reduce_scatter | solution.py:33
  72.8 1.5 copy-start.3
  72.8 80.2 %copy-start.4 = (f32[1,256]{1,0:T(1,128)S(1)}, f32[1,256]{1,0:T(1,128)}, u32[]{:S(2)}) copy-start(f32[1,256]{1,0:T(1,128)} %param.11) | copy-start | bytes 3076
  72.9 159.8 %all-gather.5.cloned.1.call-start = ((), (), s32[]{:S(2)}) async-start(), calls=%async_computation.5 | async-start | bytes 5242880 | tf_op jit(solution)/shard_map/all_gather | solution.py:44
  73.6 239.9 %all-gather.3.cloned.1.call-start = ((), (), s32[]{:S(2)}) async-start(), calls=%async_computation.4 | async-start | bytes 5242880 | tf_op jit(solution)/shard_map/all_gather | solution.py:51
  152.3 196.6 %all-reduce.3.cloned.1.call-start = ((), (), s32[]{:S(2)}) async-start(), calls=%async_computation.6 | async-start | bytes 262144 | tf_op jit(solution)/shard_map/psum | solution.py:43
  158.1 79.4 %copy-start.1 = (bf16[2048,1,256]{2,0,1:T(8,128)(2,1)S(1)}, bf16[2048,1,256]{2,0,1:T(8,128)(2,1)}, u32[]{:S(2)}) copy-start(bf16[2048,1,256]{2,0,1:T(8,128)(2,1)} %multiply_convert_fusion.1) | copy-start | bytes 3145732
  158.1 79.4 %copy-start.2 = (bf16[1,2048,256]{2,1,0:T(8,128)(2,1)S(1)}, bf16[1,2048,256]{2,1,0:T(8,128)(2,1)}, u32[]{:S(2)}) copy-start(bf16[1,2048,256]{2,1,0:T(8,128)(2,1)} %param.9) | copy-start | bytes 3145732
Sparse Core Ops, SparseCore 0:
  73.0 76.7 reduce-scatter.1
  151.4 81.2 all-gather.4
  234.2 79.2 all-gather.2
  315.7 33.1 all-reduce.2
